TPU v7x, 256 devices: a whole 4x4x8 slice. The times are simulated.
256 devices in a mesh: seq: 32 (over z, x), head: 2 (over core), batch: 4 (over y).
Axes of the slice: x: 4, y: 4, z: 8, core: 2. Of those that a mesh axis runs over, the one named last changes fastest.
Arguments:
- queries: bfloat16 [131072, 8, 256], P(('batch', 'seq'), 'head'), parts along dimension 0, may hold values from -6 to 6
- keys: bfloat16 [131072, 8, 256], P(('batch', 'seq'), 'head'), parts along dimension 0, may hold values from -0.375 to 0.375
- content_vectors: bfloat16 [131072, 8, 256], P(('batch', 'seq'), 'head'), parts along dimension 0, may hold values from -6 to 6
- decay_rate: float32 [8, 131072], P('head', ('batch', 'seq')), parts along dimension 1, may hold values from 0 to 3
- gate_pre: bfloat16 [131072, 2048], P(('batch', 'seq'), 'head'), parts along dimension 0, may hold values from -6 to 6
- norm_gain: float32 [2048], P('head'), may hold values from 0.1 to 1.9
- out_weight: bfloat16 [2048, 4096], P('head'), may hold values from -0.125 to 0.125
Outputs:
- layer_out: bfloat16 [131072, 4096], P(('batch', 'seq'), 'head'), parts along dimension 0
There are 4 independent parts, one for each index of `batch`. A program takes and returns all parts, laid end to end along the dimension named above; an argument that names none is the same for every part. Nothing has to cross between parts.
All inputs are finite; a program needn't handle non-finite values.
Results may differ from a plain program's by a relative error of at most 0.013.
Values may be sent and summed in bfloat16 or wider, within the bound.
A program may use at most 128 MiB of HBM per device.

v0:
```python
import jax
import jax.numpy as jnp
from jax import lax
from jax.sharding import PartitionSpec as P


def joined_along(tiles, dim):
    shape = list(tiles.shape[1:])
    shape[dim] *= tiles.shape[0]
    return jnp.moveaxis(tiles, 0, dim).reshape(shape)


def sent_to_all(value, axis):
    devices = lax.axis_size(axis)
    return lax.all_to_all(
        jnp.broadcast_to(value[None], (devices, *value.shape)), axis, 0, 0, tiled=True
    )


def gathered_copies(value, axis, dim):
    return joined_along(sent_to_all(value, axis), dim)


def partner_2(value, axis, bit):
    mask = 2**bit
    pairs = [(source, source ^ mask) for source in range(lax.axis_size(axis))]
    return lax.ppermute(value, axis, pairs)


def transpose_prefix(totals, segment_retained_matrix):
    devices = lax.axis_size("seq")
    every_total = gathered_copies(totals[None, :], "seq", 0)
    before = jnp.cumsum(every_total, axis=0) - every_total
    target = jnp.arange(devices)[:, None]
    source = jnp.arange(devices)[None, :]
    exponent = before.T[:, :, None] - before.T[:, None, :] - every_total.T[:, None, :]
    factors = jnp.exp(jnp.where((source < target)[None], exponent, -jnp.inf))
    aggregate_result = jnp.einsum(
        "hde,herv->hdrv",
        factors,
        lax.all_to_all(
            segment_retained_matrix[:, None], "seq", split_axis=2, concat_axis=1, tiled=True
        ),
    )
    gathered = lax.all_to_all(
        aggregate_result.astype(jnp.bfloat16), "seq", split_axis=1, concat_axis=2, tiled=True
    ).astype(aggregate_result.dtype)
    return gathered[:, 0]


def on_device(queries, keys, content_vectors, decay_rate, gate_pre, norm_gain, out_weight):
    length = queries.shape[0]
    local_heads = queries.shape[1]
    value_width = content_vectors.shape[2]
    within = -jnp.cumsum(decay_rate, axis=1)
    totals = within[:, -1]
    lookup_vectors_weighted = (jnp.exp(totals[None, :] - within.T)[:, :, None] * keys).astype(
        jnp.bfloat16
    )
    segment_retained_matrix = jnp.einsum(
        "gdj,gdl->djl", lookup_vectors_weighted, content_vectors, preferred_element_type=jnp.float32
    )
    arriving_state = transpose_prefix(totals, segment_retained_matrix)
    arriving_state_rounded = arriving_state.astype(jnp.bfloat16)
    passed_forward = jnp.einsum(
        "qaw,awi->qai", queries, arriving_state_rounded, preferred_element_type=jnp.float32
    )
    passed_forward = passed_forward * jnp.exp(within.T)[:, :, None]
    scores = jnp.einsum("lhk,shk->hls", queries, keys, preferred_element_type=jnp.float32)
    token_positions = jnp.arange(length)
    causal = token_positions[:, None] >= token_positions[None, :]
    exponent = jnp.where(causal[None], within[:, :, None] - within[:, None, :], -jnp.inf)
    weights = (scores * jnp.exp(exponent)).astype(jnp.bfloat16)
    within_block = jnp.einsum(
        "hls,shv->lhv", weights, content_vectors, preferred_element_type=jnp.float32
    )
    retained = passed_forward + within_block
    center = jnp.mean(retained, axis=2, keepdims=True)
    shifted = retained - center
    variance = jnp.mean(shifted * shifted, axis=2, keepdims=True)
    normed = (shifted * lax.rsqrt(variance + 1e-06)).reshape(length, local_heads * value_width)
    gated_rows = (normed * norm_gain * jax.nn.silu(gate_pre.astype(jnp.float32))).astype(
        jnp.bfloat16
    )
    columns = out_weight.shape[1] // 2
    head_index = lax.axis_index("head")
    own_part = lax.dynamic_slice_in_dim(out_weight, head_index * columns, columns, 1)
    other_part = lax.dynamic_slice_in_dim(out_weight, (1 - head_index) * columns, columns, 1)
    received = partner_2(other_part, "head", 0)
    partner = partner_2(gated_rows, "head", 0)
    result = jnp.dot(gated_rows, own_part, preferred_element_type=jnp.float32) + jnp.dot(
        partner, received, preferred_element_type=jnp.float32
    )
    return result.astype(jnp.bfloat16)


def solution(mesh):
    in_specs = (
        P(("batch", "seq"), "head", None),
        P(("batch", "seq"), "head", None),
        P(("batch", "seq"), "head", None),
        P("head", ("batch", "seq")),
        P(("batch", "seq"), "head"),
        P("head"),
        P("head", None),
    )
    out_specs = P(("batch", "seq"), "head")
    return jax.shard_map(
        on_device, mesh=mesh, in_specs=in_specs, out_specs=out_specs, check_vma=False
    )
```

profile of v0, /device:TPU:1, one launch (start us, length us, event | category | flops | bytes accessed | tf_op | source)
XLA Modules:
  0.0 108.2 jit_solution(6782485871576420483)
XLA Ops:
  0.0 0.9 copy.108
  0.9 1.1 %reduce-window.6 = f32[4,8,128]{2,1,0:T(8,128)S(1)} reduce-window(f32[4,8,128]{2,1,0:T(8,128)S(1)} %bitcast.51, f32[]{:T(128)} %constant.9.clone.1), window={size=1x1x128 pad=0_0x0_0x127_0}, to_apply=%region_0.0 | reduce-window | flops 520192 | bytes 32772 | tf_op jit(solution)/shard_map/reduce-window
  3.2 11.9 %all-to-all-start = ((f32[32,1,4]{2,1,0:T(1,128)}), f32[32,1,4]{2,1,0:T(1,128)S(1)}, u32[]{:S(2)}, u32[]{:S(2)}) async-start(f32[32,1,4]{2,1,0:T(1,128)} %broadcast_in_dim.28), calls=%async_computation | async-start | bytes 32768 | tf_op jit(solution)/shard_map/all_to_all | solution.py:15
  15.4 4.3 %copy.70 = bf16[1024,4,256]{0,2,1:T(8,128)(2,1)} copy(bf16[1024,4,256]{2,1,0:T(4,128)(2,1)} %param.9) | data formatting | bytes 4194304 | tf_op args[2]
  19.7 2.4 %multiply_convert_fusion.1 = bf16[1024,4,256]{2,1,0:T(4,128)(2,1)S(1)} fusion(bf16[1024,4,256]{2,1,0:T(4,128)(2,1)S(1)} %copy-done, f32[1024,4]{1,0:T(8,128)S(1)} %copy.58), kind=kLoop, calls=%fused_computation.14 | loop fusion | flops 3145728 | bytes 4210688 | tf_op jit(solution)/shard_map/convert_element_type | solution.py:57
  22.1 0.9 fusion.15
  23.0 1.2 %copy.61 = bf16[4,1,256,256]{3,0,1,2:T(4,128)(2,1)} copy(bf16[4,1,256,256]{3,2,0,1:T(8,128)(2,1)S(1)} %fusion.15) | data formatting | bytes 1048576 | tf_op jit(solution)/shard_map/broadcast_in_dim | solution.py:42
  24.2 9.2 %all-to-all-start.1 = ((bf16[4,1,256,256]{3,0,1,2:T(4,128)(2,1)}), bf16[4,1,256,256]{3,0,1,2:T(4,128)(2,1)S(1)}, u32[]{:S(2)}, u32[]{:S(2)}) async-start(bf16[4,1,256,256]{3,0,1,2:T(4,128)(2,1)} %copy.61), calls=%async_computation.1 | async-start | bytes 1048576 | tf_op jit(solution)/shard_map/all_to_all | solution.py:41
  33.5 4.7 %constant_dynamic-slice_fusion = bf16[1024,2048]{1,0:T(8,128)(2,1)} fusion(bf16[1024,4096]{1,0:T(8,128)(2,1)} %param.13, s32[]{:T(128)S(6)} %select_n.17), kind=kLoop, calls=%fused_computation.48 | loop fusion | bytes 8388612 | tf_op jit(solution)/shard_map/dynamic_slice | solution.py:88
  38.2 1.5 %collective-permute-start.1 = (bf16[1024,2048]{1,0:T(8,128)(2,1)}, bf16[1024,2048]{1,0:T(8,128)(2,1)}, u32[]{:S(2)}, u32[]{:S(2)}) collective-permute-start(bf16[1024,2048]{1,0:T(8,128)(2,1)} %constant_dynamic-slice_fusion), channel_id=1, source_target_pairs={{0,4},{4,0},{1,5},{5,1},{2,6},{6,2},{3,7},{7,3},{8,12},{12,8},{9,1... | collective-permute-start | bytes 12582920 | tf_op jit(solution)/shard_map/ppermute | solution.py:27
  39.7 1.3 %iota_compare_fusion = pred[1024,1024]{1,0:T(8,128)(4,1)} fusion(), kind=kLoop, calls=%fused_computation.13 | loop fusion | flops 1048576 | bytes 1048576 | tf_op jit(solution)/shard_map/ge | solution.py:71
  41.3 7.6 %all-to-all-done.1 = bf16[4,1,256,256]{3,0,1,2:T(4,128)(2,1)S(1)} async-done(((bf16[4,1,256,256]{3,0,1,2:T(4,128)(2,1)}), bf16[4,1,256,256]{3,0,1,2:T(4,128)(2,1)S(1)}, u32[]{:S(2)}, u32[]{:S(2)}) %all-to-all-start.1) | async-done | bytes 524320 | tf_op jit(solution)/shard_map/all_to_all | solution.py:41
  48.9 0.8 convolution_convert_fusion
  49.7 1.1 %copy.64 = bf16[4,32,8,256]{3,2,0,1:T(8,128)(2,1)} copy(bf16[4,32,8,256]{3,1,2,0:T(8,128)(2,1)S(1)} %convolution_convert_fusion) | data formatting | bytes 1048576 | tf_op jit(solution)/shard_map/convert_element_type | solution.py:46
  50.8 6.3 %all-to-all-start.2 = ((bf16[4,32,8,256]{3,2,0,1:T(8,128)(2,1)}), bf16[4,32,8,256]{3,2,0,1:T(8,128)(2,1)S(1)}, u32[]{:S(2)}, u32[]{:S(2)}) async-start(bf16[4,32,8,256]{3,2,0,1:T(8,128)(2,1)} %copy.64), calls=%async_computation.2 | async-start | bytes 1048576 | tf_op jit(solution)/shard_map/all_to_all | solution.py:45
  57.1 10.7 %fusion.7 = f32[4,1024,256]{1,2,0:T(8,128)} fusion(bf16[1024,4,256]{0,2,1:T(8,128)(2,1)} %copy.70, f32[4,1024]{1,0:T(4,128)S(1)} %bitcast.53, pred[1024,1024]{1,0:T(8,128)(4,1)} %iota_compare_fusion, bf16[1024,4,256]{2,1,0:T(4,128)(2,1)S(1)} %copy-done, bf16[1024,4,256]{2,1,0:T(4,128)(2,1)} %param.7), kind=kOutput, calls=%fused_computation.17 | convolution fusion | flops 4311744512 | bytes 11550720 | tf_op jit(solution)/shard_map/hls,shv->lhv/dot_general | solution.py:74
  67.8 4.4 %all-to-all-done.2 = bf16[4,32,8,256]{3,2,0,1:T(8,128)(2,1)S(1)} async-done(((bf16[4,32,8,256]{3,2,0,1:T(8,128)(2,1)}), bf16[4,32,8,256]{3,2,0,1:T(8,128)(2,1)S(1)}, u32[]{:S(2)}, u32[]{:S(2)}) %all-to-all-start.2) | async-done | bytes 524320 | tf_op jit(solution)/shard_map/all_to_all | solution.py:45
  72.1 3.9 %fusion.34 = (f32[1024,4]{0,1:T(4,128)S(1)}, f32[1024,4,256]{0,2,1:T(8,128)S(1)}) fusion(f32[4,1024,256]{1,2,0:T(8,128)} %fusion.7, f32[1024,4]{0,1:T(4,128)S(1)} %get-tuple-element.6, bf16[1024,4,256]{2,1,0:T(4,128)(2,1)} %param.7, bf16[4,32,8,256]{3,2,0,1:T(8,128)(2,1)S(1)} %all-to-all-done.2), kind=kOutput, calls=%fused_computation.52 | convolution fusion | flops 540012544 | bytes 11042816 | tf_op jit(solution)/shard_map/qaw,awi->qai/dot_general | solution.py:65
  76.6 2.5 %subtract_multiply_fusion = f32[1024,4,256]{0,2,1:T(8,128)} fusion(f32[1024,4,256]{0,2,1:T(8,128)S(1)} %get-tuple-element.8, f32[1024,4]{0,1:T(4,128)S(1)} %add_rsqrt_fusion, f32[1024,4]{0,1:T(4,128)S(1)} %broadcast_multiply_fusion), kind=kLoop, calls=%fused_computation.16 | loop fusion | flops 2097152 | bytes 8421376 | tf_op jit(solution)/shard_map/mul | solution.py:81
  79.2 5.5 %copy.71 = f32[1024,1024]{1,0:T(8,128)} copy(f32[1024,1024]{0,1:T(8,128)} %bitcast.49) | data formatting | bytes 8388608 | tf_op jit(solution)/shard_map/reshape | solution.py:81
  84.7 4.8 %fusion.6 = bf16[1024,1024]{1,0:T(8,128)(2,1)} fusion(bf16[1024,1024]{1,0:T(8,128)(2,1)S(1)} %copy-done.2, f32[1024,1024]{1,0:T(8,128)} %copy.71, f32[1024]{0:T(1024)S(1)} %copy-done.3), kind=kLoop, calls=%fused_computation.15 | loop fusion | flops 8388608 | bytes 8392704 | tf_op jit(solution)/shard_map/convert_element_type | solution.py:82
  89.4 3.6 %collective-permute-start = (bf16[1024,1024]{1,0:T(8,128)(2,1)}, bf16[1024,1024]{1,0:T(8,128)(2,1)S(1)}, u32[]{:S(2)}, u32[]{:S(2)}) collective-permute-start(bf16[1024,1024]{1,0:T(8,128)(2,1)} %fusion.6), channel_id=1, source_target_pairs={{0,4},{4,0},{1,5},{5,1},{2,6},{6,2},{3,7},{7,3},{8,12},{12,8},{9,1... | collective-permute-start | bytes 6291464 | tf_op jit(solution)/shard_map/ppermute | solution.py:27
  93.0 6.9 %fusion.4 = f32[1024,2048]{1,0:T(8,128)S(1)} fusion(bf16[1024,1024]{1,0:T(8,128)(2,1)} %fusion.6, bf16[1024,4096]{1,0:T(8,128)(2,1)} %param.13, s32[]{:T(128)S(6)} %select_n.16), kind=kOutput, calls=%fused_computation.10 | convolution fusion | flops 4294967296 | bytes 14680068 | tf_op jit(solution)/shard_map/dot_general | solution.py:91
  100.0 8.2 %add_convert_fusion = bf16[1024,2048]{1,0:T(8,128)(2,1)} fusion(f32[1024,2048]{1,0:T(8,128)S(1)} %fusion.4, bf16[1024,1024]{1,0:T(8,128)(2,1)S(1)} %collective-permute-done, bf16[1024,2048]{1,0:T(8,128)(2,1)} %collective-permute-done.1), kind=kOutput, calls=%fused_computation.1 | convolution fusion | flops 4299161600 | bytes 18874368 | tf_op jit(solution)/shard_map/dot_general | solution.py:91
  (29 shorter events, 2.4 us)
Async XLA Ops:
  0.0 19.7 %copy-start = (bf16[1024,4,256]{2,1,0:T(4,128)(2,1)S(1)}, bf16[1024,4,256]{2,1,0:T(4,128)(2,1)}, u32[]{:S(2)}) copy-start(bf16[1024,4,256]{2,1,0:T(4,128)(2,1)} %param.8) | copy-start | bytes 6291460
  3.2 21.0 %all-to-all-start = ((f32[32,1,4]{2,1,0:T(1,128)}), f32[32,1,4]{2,1,0:T(1,128)S(1)}, u32[]{:S(2)}, u32[]{:S(2)}) async-start(f32[32,1,4]{2,1,0:T(1,128)} %broadcast_in_dim.28), calls=%async_computation | async-start | bytes 32768 | tf_op jit(solution)/shard_map/all_to_all | solution.py:15
  19.7 2.4 %copy-start.1 = (bf16[1024,4,256]{0,2,1:T(8,128)(2,1)S(1)}, bf16[1024,4,256]{0,2,1:T(8,128)(2,1)}, u32[]{:S(2)}) copy-start(bf16[1024,4,256]{0,2,1:T(8,128)(2,1)} %copy.70) | copy-start | bytes 6291460
  24.2 24.6 %all-to-all-start.1 = ((bf16[4,1,256,256]{3,0,1,2:T(4,128)(2,1)}), bf16[4,1,256,256]{3,0,1,2:T(4,128)(2,1)S(1)}, u32[]{:S(2)}, u32[]{:S(2)}) async-start(bf16[4,1,256,256]{3,0,1,2:T(4,128)(2,1)} %copy.61), calls=%async_computation.1 | async-start | bytes 1048576 | tf_op jit(solution)/shard_map/all_to_all | solution.py:41
  38.2 61.8 %collective-permute-start.1 = (bf16[1024,2048]{1,0:T(8,128)(2,1)}, bf16[1024,2048]{1,0:T(8,128)(2,1)}, u32[]{:S(2)}, u32[]{:S(2)}) collective-permute-start(bf16[1024,2048]{1,0:T(8,128)(2,1)} %constant_dynamic-slice_fusion), channel_id=1, source_target_pairs={{0,4},{4,0},{1,5},{5,1},{2,6},{6,2},{3,7},{7,3},{8,12},{12,8},{9,1... | collective-permute-start | bytes 12582920 | tf_op jit(solution)/shard_map/ppermute | solution.py:27
  50.8 21.4 %all-to-all-start.2 = ((bf16[4,32,8,256]{3,2,0,1:T(8,128)(2,1)}), bf16[4,32,8,256]{3,2,0,1:T(8,128)(2,1)S(1)}, u32[]{:S(2)}, u32[]{:S(2)}) async-start(bf16[4,32,8,256]{3,2,0,1:T(8,128)(2,1)} %copy.64), calls=%async_computation.2 | async-start | bytes 1048576 | tf_op jit(solution)/shard_map/all_to_all | solution.py:45
  79.2 5.5 %copy-start.2 = (bf16[1024,1024]{1,0:T(8,128)(2,1)S(1)}, bf16[1024,1024]{1,0:T(8,128)(2,1)}, u32[]{:S(2)}) copy-start(bf16[1024,1024]{1,0:T(8,128)(2,1)} %param.11) | copy-start | bytes 6291460
  79.2 5.5 %copy-start.3 = (f32[1024]{0:T(1024)S(1)}, f32[1024]{0:T(1024)}, u32[]{:S(2)}) copy-start(f32[1024]{0:T(1024)} %param.12) | copy-start | bytes 12292
  89.4 10.5 %collective-permute-start = (bf16[1024,1024]{1,0:T(8,128)(2,1)}, bf16[1024,1024]{1,0:T(8,128)(2,1)S(1)}, u32[]{:S(2)}, u32[]{:S(2)}) collective-permute-start(bf16[1024,1024]{1,0:T(8,128)(2,1)} %fusion.6), channel_id=1, source_target_pairs={{0,4},{4,0},{1,5},{5,1},{2,6},{6,2},{3,7},{7,3},{8,12},{12,8},{9,1... | collective-permute-start | bytes 6291464 | tf_op jit(solution)/shard_map/ppermute | solution.py:27
where the time goes:
time: 109 us; the launch traced here: 108 us
  starting transfers between devices  32.5 us (30%)
  matrix products  31.4 us (29%)
  local copies, waits for them, and re-layouts  19.1 us (18%)
  other arithmetic  13.1 us (12%)
  waiting for transfers between devices  11.9 us (11%)
    all_to_all x1, starting transfers between devices, sent_to_all(): lax.all_to_all(jnp.broadcast_to(value[None], (devices, *value.shape)), ax...  11.9 us
    dot_general x1, matrix products, on_device(): jnp.einsum('hls,shv->lhv', weights, content_vectors, preferred_element_ty...  10.7 us
    all_to_all x1, starting transfers between devices, transpose_prefix(): lax.all_to_all(segment_retained_matrix[:, None], 'seq', split_axis=2, con...  9.22 us
    dot_general x1, matrix products, on_device(): jnp.dot(partner, received, preferred_element_type=jnp.float32)  8.22 us
    all_to_all x1, waiting for transfers between devices, transpose_prefix(): lax.all_to_all(segment_retained_matrix[:, None], 'seq', split_axis=2, con...  7.57 us
    dot_general x1, matrix products, on_device(): jnp.dot(gated_rows, own_part, preferred_element_type=jnp.float32)  6.92 us
    all_to_all x1, starting transfers between devices, transpose_prefix(): lax.all_to_all(aggregate_result.astype(jnp.bfloat16), 'seq', split_axis=1...  6.31 us
    reshape x1, local copies, waits for them, and re-layouts, on_device(): (shifted * lax.rsqrt(variance + 1e-06)).reshape(length, local_heads * val...  5.49 us
  transfers between devices with their start and end apart: 5, of which 2 were waited for; matrix products, arithmetic and copies ran while one was open for 48% of the time, Pallas kernels for 0%

commit v1 on v0

v1 whole, which is shorter than its diff:
```python
import jax
import jax.numpy as jnp
from jax import lax
from jax.experimental import pallas as pl
from jax.experimental.pallas import tpu as pltpu
from jax.sharding import PartitionSpec as P

NX, NZ = 4, 8
TOK, HL, DH = 1024, 4, 256
COLS = 2048
QR = DH // NX
PR, PC = 16, 128
TB = 256
BF, F32 = jnp.bfloat16, jnp.float32
MESH = pl.DeviceIdType.MESH


def kernel(
    q_hbm, k_hbm, v_hbm, d_hbm, gate_hbm, gain_ref, w_hbm, o_hbm,
    raw, kp, vp, qp, dec, gate, gfac, wcat, gcat, acc, ostage, within,
    perm, wrow, wcol, sb, xs, ab, zr, i0s, i0r, ins, inr,
    tsend, txr, etx, tzsend, tzr, etz,
    lsem, wsem, tx_s, tx_r, tz_s, tz_r, s1_s, s1_r, s2_s, s2_r, s3_s, s3_r, s4_s, s4_r,
    g_s, g_r, wr_s, wr_r, osem,
):
    seq = lax.axis_index("seq")
    core = lax.axis_index("head")
    x = lax.rem(seq, NX)
    z = lax.div(seq, NX)

    def x_peer(d):
        return lax.rem(x + d, NX)

    def z_peer(d):
        return lax.rem(z + d, NZ)

    def at_x(d):
        return {"seq": z * NX + x_peer(d)}

    def at_z(d):
        return {"seq": z_peer(d) * NX + x}

    partner = {"head": 1 - core}

    barrier = pltpu.get_barrier_semaphore()
    for d in range(1, NX):
        pl.semaphore_signal(barrier, inc=1, device_id=at_x(d), device_id_type=MESH)
    for d in range(1, NZ):
        pl.semaphore_signal(barrier, inc=1, device_id=at_z(d), device_id_type=MESH)
    pl.semaphore_signal(barrier, inc=1, device_id=partner, device_id_type=MESH)

    dcopy = pltpu.make_async_copy(d_hbm, dec, lsem.at[12])
    dcopy.start()
    ld = {}
    for n, (src, slot) in enumerate(((k_hbm, 0), (v_hbm, 1), (q_hbm, 2))):
        for c in range(4):
            rows = pl.ds(c * TB, TB)
            ld[n, c] = pltpu.make_async_copy(src.at[rows], raw.at[slot, rows], lsem.at[n * 4 + c])
    for n in (0, 1):
        for c in range(4):
            ld[n, c].start()
    gcopy = pltpu.make_async_copy(gate_hbm, gate, lsem.at[13])

    def remote(src, dst, ss, rs, dev):
        return pltpu.make_async_remote_copy(
            src_ref=src, dst_ref=dst, send_sem=ss, recv_sem=rs, device_id=dev, device_id_type=MESH
        )

    own_cols = pl.ds(pl.multiple_of(core * COLS, COLS), COLS)
    other_cols = pl.ds(pl.multiple_of((1 - core) * COLS, COLS), COLS)
    w_local, w_far = [], []
    for h in range(HL):
        rows = pl.ds(h * DH, DH)
        w_local.append(
            pltpu.make_async_copy(
                w_hbm.at[rows, own_cols], wcat.at[pl.ds(h * 2 * DH, DH)], wsem.at[h]
            )
        )
        w_far.append(
            remote(
                w_hbm.at[rows, other_cols], wcat.at[pl.ds(h * 2 * DH + DH, DH)],
                wr_s.at[h], wr_r.at[h], partner,
            )
        )

    ri = lax.broadcasted_iota(jnp.int32, (256, 256), 0)
    ci = lax.broadcasted_iota(jnp.int32, (256, 256), 1)
    perm[...] = jnp.where(ci == HL * (ri % 64) + ri // 64, 1.0, 0.0).astype(BF)

    ui = lax.broadcasted_iota(jnp.int32, (128, 256), 0)
    uj = lax.broadcasted_iota(jnp.int32, (128, 256), 1)
    upper = jnp.where(ui <= uj, 1.0, 0.0).astype(F32)
    dcopy.wait()
    stacked = jnp.concatenate([dec[:, c * 128:(c + 1) * 128] for c in range(8)], axis=0)
    sums = jnp.dot(stacked, upper, precision=lax.Precision.HIGHEST, preferred_element_type=F32)
    off = jnp.zeros((HL, 128), F32)
    parts = []
    for c in range(8):
        parts.append(-(off + sums[c * HL:(c + 1) * HL, :128]))
        off = off + sums[c * HL:(c + 1) * HL, 128:]
    w4 = jnp.concatenate(parts, axis=1)
    tot = -off
    tot8 = jnp.concatenate([tot] * 8, axis=1)
    ek = jnp.exp(tot8 - w4)
    eq = jnp.exp(w4)
    rows16 = jnp.concatenate([w4, ek, eq, eq], axis=0)
    wrow[...] = rows16
    wcol[...] = rows16.T
    tt = jnp.concatenate([tot, tot], axis=1)
    tsend[...] = jnp.concatenate([tt, tt], axis=0)
    txr[x] = tsend[...]

    pl.semaphore_wait(barrier, NX - 1 + NZ - 1 + 1)
    tx = [
        remote(tsend, txr.at[x], tx_s.at[d - 1], tx_r.at[d - 1], at_x(d)) for d in range(1, NX)
    ]
    for c in tx:
        c.start()

    def permute(n, dst):
        for c in range(4):
            ld[n, c].wait()
            for b in range(4):
                p0 = c * TB + b * 64
                r = jnp.dot(
                    perm[...], raw[n, p0:p0 + 64].reshape(256, 256), preferred_element_type=F32
                ).astype(BF)
                for h in range(HL):
                    dst[h, p0:p0 + 64, :] = r[h * 64:(h + 1) * 64]

    permute(0, kp)
    permute(1, vp)
    for c in range(4):
        ld[2, c].start()
    gcopy.start()
    for h in range(HL):
        w_local[h].start()
        w_far[h].start()

    s1 = {}
    for h in range(HL):
        scaled = (kp[h].astype(F32) * wcol[:, HL + h:HL + h + 1]).astype(BF)
        state = lax.dot_general(
            scaled, vp[h], (((0,), (0,)), ((), ())), preferred_element_type=F32
        ).astype(BF)
        for r in range(NX):
            sb[h, r] = state[r * QR:(r + 1) * QR]
        xs[h, x] = sb[h, x]
        for d in (1, 3, 2):
            s1[h, d] = remote(
                sb.at[h, x_peer(d)], xs.at[h, x], s1_s.at[h, d - 1], s1_r.at[h, d - 1], at_x(d)
            )
            s1[h, d].start()

    permute(2, qp)

    for c in tx:
        c.wait_recv()
    row_total = txr[0] + txr[1] + txr[2] + txr[3]
    tzsend[...] = row_total
    tzr[z] = row_total
    etx[...] = jnp.exp(txr[...])
    tz = [
        remote(tzsend, tzr.at[z], tz_s.at[d - 1], tz_r.at[d - 1], at_z(d)) for d in range(1, NZ)
    ]
    for c in tz:
        c.start()

    ti = lax.broadcasted_iota(jnp.int32, (TB, TB), 0)
    si = lax.broadcasted_iota(jnp.int32, (TB, TB), 1)

    def do_within(h):
        for tb in range(TOK // TB):
            t0 = tb * TB
            n = t0 + TB
            s = lax.dot_general(
                qp[h, t0:n, :], kp[h, :n, :], (((1,), (1,)), ((), ())), preferred_element_type=F32
            )
            wt = wcol[t0:n, h:h + 1]
            diag = jnp.where(ti >= si, wt - wrow[h:h + 1, t0:n], -jnp.inf)
            p = (s[:, t0:] * jnp.exp(diag)).astype(BF)
            if tb > 0:
                far = (s[:, :t0] * jnp.exp(wt - wrow[h:h + 1, :t0])).astype(BF)
                p = jnp.concatenate([far, p], axis=1)
            within[h, t0:n, :] = jnp.dot(p, vp[h, :n, :], preferred_element_type=F32)

    s2, s3, s4 = {}, {}, {}

    def stage_a(h):
        for d in range(1, NX):
            s1[h, d].wait_recv()
        a = xs[h, 0].astype(F32)
        for i in range(1, NX):
            a = a * etx[i, h:h + 1, :] + xs[h, i].astype(F32)
        a = a.astype(BF)
        for r in range(4):
            for c in range(2):
                ab[h, r + 4 * c] = a[r * PR:(r + 1) * PR, c * PC:(c + 1) * PC]
        zr[h, z] = ab[h, z]
        for d in (4, 3, 5, 2, 6, 1, 7):
            s2[h, d] = remote(
                ab.at[h, z_peer(d)], zr.at[h, z], s2_s.at[h, d - 1], s2_r.at[h, d - 1], at_z(d)
            )
            s2[h, d].start()

    def stage_z(h):
        for d in range(1, NZ):
            s2[h, d].wait_recv()
        run = zr[h, 0].astype(F32)
        i0s[h, 0] = jnp.zeros((PR, PC), BF)
        i0s[h, 1] = run.astype(BF)
        for i in range(1, NZ - 1):
            run = run * etz[i, h:h + 1, :PC] + zr[h, i].astype(F32)
            i0s[h, i + 1] = run.astype(BF)
        i0r[h, z] = i0s[h, z]
        for d in (4, 3, 5, 2, 6, 1, 7):
            s3[h, d] = remote(
                i0s.at[h, z_peer(d)], i0r.at[h, z], s3_s.at[h, d - 1], s3_r.at[h, d - 1], at_z(d)
            )
            s3[h, d].start()

    def stage_x(h):
        for d in range(1, NZ):
            s3[h, d].wait_recv()
        for r in range(4):
            for c in range(2):
                rows, cols = slice(r * PR, (r + 1) * PR), slice(c * PC, (c + 1) * PC)
                run = i0r[h, r + 4 * c].astype(F32)
                ins[h, 0, rows, cols] = run.astype(BF)
                for i in range(NX - 1):
                    run = run * etx[i, h:h + 1, cols] + xs[h, i, rows, cols].astype(F32)
                    ins[h, i + 1, rows, cols] = run.astype(BF)
        inr[h, x] = ins[h, x]
        for d in (2, 1, 3):
            s4[h, d] = remote(
                ins.at[h, x_peer(d)], inr.at[h, x], s4_s.at[h, d - 1], s4_r.at[h, d - 1], at_x(d)
            )
            s4[h, d].start()

    for h in range(HL):
        do_within(h)
        stage_a(h)

    for c in tz:
        c.wait_recv()
    etz[...] = jnp.exp(tzr[...])

    gcopy.wait()

    def gate_factor(h):
        cols = slice(h * DH, (h + 1) * DH)
        gp = gate[:, cols].astype(F32)
        gfac[:, cols] = gain_ref[:, cols] * (gp / (1.0 + jnp.exp(-gp)))

    for h in range(HL):
        gate_factor(h)
        stage_z(h)
    for h in range(HL):
        stage_x(h)

    gx = {}

    def finalize(h):
        for d in range(1, NX):
            s4[h, d].wait_recv()
        inc = inr[h].reshape(DH, DH)
        for tb in range(TOK // TB):
            rows = slice(tb * TB, (tb + 1) * TB)
            ret = jnp.dot(qp[h, rows, :], inc, preferred_element_type=F32)
            ret = ret * wcol[rows, 2 * HL + h:2 * HL + h + 1] + within[h, rows, :]
            center = jnp.mean(ret, axis=1, keepdims=True)
            shifted = ret - center
            variance = jnp.mean(shifted * shifted, axis=1, keepdims=True)
            normed = shifted * lax.rsqrt(variance + 1e-06)
            gcat[rows, h * 2 * DH:h * 2 * DH + DH] = (
                normed * gfac[rows, h * DH:(h + 1) * DH]
            ).astype(BF)
            rr = pl.ds(tb * TB, TB)
            gx[h, tb] = remote(
                gcat.at[rr, pl.ds(h * 2 * DH, DH)], gcat.at[rr, pl.ds(h * 2 * DH + DH, DH)],
                g_s.at[h, tb], g_r.at[h, tb], partner,
            )
            gx[h, tb].start()

    oc = []

    def project(h):
        w_local[h].wait()
        w_far[h].wait_recv()
        for tb in range(TOK // TB):
            gx[h, tb].wait_recv()
        depth = slice(h * 2 * DH, (h + 1) * 2 * DH)
        for j in range(COLS // 256):
            cols = slice(j * 256, (j + 1) * 256)
            part = jnp.dot(gcat[:, depth], wcat[depth, cols], preferred_element_type=F32)
            if h == 0:
                acc[:, cols] = part
            elif h < HL - 1:
                acc[:, cols] += part
            else:
                ostage[:, cols] = (acc[:, cols] + part).astype(BF)
                c = pltpu.make_async_copy(
                    ostage.at[:, pl.ds(j * 256, 256)], o_hbm.at[:, pl.ds(j * 256, 256)], osem.at[j]
                )
                c.start()
                oc.append(c)

    finalize(0)
    finalize(1)
    project(0)
    finalize(2)
    project(1)
    finalize(3)
    project(2)
    project(3)

    for group in (s1, s2, s3, s4, gx):
        for c in group.values():
            c.wait_send()
    for group in (tx, tz, w_far):
        for c in group:
            c.wait_send()
    for c in oc:
        c.wait()


def on_device(queries, keys, content_vectors, decay_rate, gate_pre, norm_gain, out_weight):
    hbm = pl.BlockSpec(memory_space=pl.ANY)
    vmem = pl.BlockSpec(memory_space=pltpu.VMEM)
    dma = pltpu.SemaphoreType.DMA
    scratch = [
        pltpu.VMEM((3, TOK, HL, DH), BF),
        pltpu.VMEM((HL, TOK, DH), BF),
        pltpu.VMEM((HL, TOK, DH), BF),
        pltpu.VMEM((HL, TOK, DH), BF),
        pltpu.VMEM((HL, TOK), F32),
        pltpu.VMEM((TOK, HL * DH), BF),
        pltpu.VMEM((TOK, HL * DH), F32),
        pltpu.VMEM((2 * HL * DH, COLS), BF),
        pltpu.VMEM((TOK, 2 * HL * DH), BF),
        pltpu.VMEM((TOK, COLS), F32),
        pltpu.VMEM((TOK, COLS), BF),
        pltpu.VMEM((HL, TOK, DH), F32),
        pltpu.VMEM((256, 256), BF),
        pltpu.VMEM((4 * HL, TOK), F32),
        pltpu.VMEM((TOK, 4 * HL), F32),
        pltpu.VMEM((HL, NX, QR, DH), BF),
        pltpu.VMEM((HL, NX, QR, DH), BF),
        pltpu.VMEM((HL, NZ, PR, PC), BF),
        pltpu.VMEM((HL, NZ, PR, PC), BF),
        pltpu.VMEM((HL, NZ, PR, PC), BF),
        pltpu.VMEM((HL, NZ, PR, PC), BF),
        pltpu.VMEM((HL, NX, QR, DH), BF),
        pltpu.VMEM((HL, NX, QR, DH), BF),
        pltpu.VMEM((8, DH), F32),
        pltpu.VMEM((NX, 8, DH), F32),
        pltpu.VMEM((NX, 8, DH), F32),
        pltpu.VMEM((8, DH), F32),
        pltpu.VMEM((NZ, 8, DH), F32),
        pltpu.VMEM((NZ, 8, DH), F32),
        dma((14,)), dma((HL,)),
        dma((NX - 1,)), dma((NX - 1,)), dma((NZ - 1,)), dma((NZ - 1,)),
        dma((HL, NX - 1)), dma((HL, NX - 1)), dma((HL, NZ - 1)), dma((HL, NZ - 1)),
        dma((HL, NZ - 1)), dma((HL, NZ - 1)), dma((HL, NX - 1)), dma((HL, NX - 1)),
        dma((HL, TOK // TB)), dma((HL, TOK // TB)), dma((HL,)), dma((HL,)), dma((COLS // 256,)),
    ]
    return pl.pallas_call(
        kernel,
        out_shape=jax.ShapeDtypeStruct((TOK, COLS), BF),
        in_specs=[hbm, hbm, hbm, hbm, hbm, vmem, hbm],
        out_specs=hbm,
        scratch_shapes=scratch,
        compiler_params=pltpu.CompilerParams(
            collective_id=0, has_side_effects=True, vmem_limit_bytes=62 * 1024 * 1024
        ),
        name="retention",
    )(queries, keys, content_vectors, decay_rate, gate_pre, norm_gain.reshape(1, -1), out_weight)


def solution(mesh):
    in_specs = (
        P(("batch", "seq"), "head", None),
        P(("batch", "seq"), "head", None),
        P(("batch", "seq"), "head", None),
        P("head", ("batch", "seq")),
        P(("batch", "seq"), "head"),
        P("head"),
        P("head", None),
    )
    out_specs = P(("batch", "seq"), "head")
    return jax.shard_map(
        on_device, mesh=mesh, in_specs=in_specs, out_specs=out_specs, check_vma=False
    )
```

time: 109 us -> 54 us (0.50)
  Pallas kernels: 0 us -> 49 us
  starting transfers between devices: 32.5 us -> 0 us
  matrix products: 31.4 us -> 0 us
  local copies, waits for them, and re-layouts: 19.1 us -> 4.79 us
  other arithmetic: 13.1 us -> 0 us
  waiting for transfers between devices: 11.9 us -> 0 us
    pallas_call x0 -> x1, Pallas kernels: none -> 49 us  [on_device(): pl.pallas_call(kernel, out_shape=jax.ShapeDtypeStruct((TOK, COLS), BF), i...]
    dot_general x6 -> x0, matrix products: 31.4 us -> none  [the longest x1 10.7 us: on_device(): jnp.einsum('hls,shv->lhv', weights, content_vectors, preferred_element_ty...]
    all_to_all x3 -> x0, starting transfers between devices: 27.4 us -> none  [the longest x1 11.9 us: sent_to_all(): lax.all_to_all(jnp.broadcast_to(value[None], (devices, *value.shape)), ax...]
    all_to_all x3 -> x0, waiting for transfers between devices: 11.9 us -> none  [the longest x1 7.57 us: transpose_prefix(): lax.all_to_all(segment_retained_matrix[:, None], 'seq', split_axis=2, con...]
    convert_element_type x2 -> x0, other arithmetic: 7.21 us -> none  [the longest x1 4.78 us: on_device(): (normed * norm_gain * jax.nn.silu(gate_pre.astype(jnp.float32))).astype(j...]
    reshape x2 -> x0, local copies, waits for them, and re-layouts: 5.58 us -> none  [the longest x1 5.49 us: on_device(): (shifted * lax.rsqrt(variance + 1e-06)).reshape(length, local_heads * val...]
    ppermute x2 -> x0, starting transfers between devices: 5.1 us -> none  [partner_2(): return lax.ppermute(value, axis, pairs)]
    dynamic_slice x1 -> x0, local copies, waits for them, and re-layouts: 4.71 us -> none  [on_device(): lax.dynamic_slice_in_dim(out_weight, (1 - head_index) * columns, columns, 1)]
  transfers between devices with their start and end apart: 5 -> 0, of which waited for: 2 -> 0; matrix products, arithmetic and copies ran while one was open for 48% -> 0% of each run, Pallas kernels for 0% -> 0%
where the time goes in v1:
time: 54 us; the launch traced here: 53.8 us
  Pallas kernels  49 us (91%)
  local copies, waits for them, and re-layouts  4.79 us (9%)
    pallas_call x1, Pallas kernels, on_device(): pl.pallas_call(kernel, out_shape=jax.ShapeDtypeStruct((TOK, COLS), BF), i...  49 us
    unnamed x1, local copies, waits for them, and re-layouts  4.79 us

profile of v1, /device:TPU:1, one launch (start us, length us, event | category | flops | bytes accessed | tf_op | source)
XLA Modules:
  0.0 53.8 jit_solution(3769877051049816491)
XLA Ops:
  0.0 49.0 %retention.1 = bf16[1024,2048]{1,0:T(8,128)(2,1)} custom-call(bf16[1024,4,256]{2,1,0:T(4,128)(2,1)} %q_hbm.1, bf16[1024,4,256]{2,1,0:T(4,128)(2,1)} %k_hbm.1, bf16[1024,4,256]{2,1,0:T(4,128)(2,1)} %v_hbm.1, f32[4,1024]{1,0:T(4,128)} %d_hbm.1, bf16[1024,1024]{1,0:T(8,128)(2,1)} %gate_hbm.1, f32[1,1024]{1,0:T(1,128)} %bitcast.1, bf16[1024,4096]{1,0:T(8,128)(2,1)} %w_hbm.1), custom_call_target="tpu_custom_call" | custom-call | tf_op jit(solution)/shard_map/retention/pallas_call | solution.py:367
  49.0 4.8 %copy.9 = bf16[1024,2048]{1,0:T(8,128)(2,1)} copy(bf16[1024,2048]{1,0:T(8,128)(2,1)} %retention.1) | data formatting | bytes 8388608

commit v2 on v1

v2 whole, which is shorter than its diff:
```python
import jax
import jax.numpy as jnp
from jax import lax
from jax.experimental import pallas as pl
from jax.experimental.pallas import tpu as pltpu
from jax.sharding import PartitionSpec as P

NX, NZ = 4, 8
TOK, HL, DH = 1024, 4, 256
COLS = 2048
QR = DH // NX
PR, PC = 16, 128
TB = 256
BF, F32 = jnp.bfloat16, jnp.float32
MESH = pl.DeviceIdType.MESH
SC = jax.named_scope
VMEM_MIB = 56


def kernel(
    q_hbm, k_hbm, v_hbm, d_hbm, gate_hbm, gain_ref, w_hbm, o_ref,
    raw, kp, ks, vp, qp, dec, gate, gfac, wcat, gcat, acc, within,
    perm, wrow, wcol, sb, xs, ab, zr, i0s, i0r, ins, inr,
    tsend, txr, etx, tzsend, tzr, etz,
    lsem, tx_s, tx_r, tz_s, tz_r, s1_s, s1_r, s2_s, s2_r, s3_s, s3_r, s4_s, s4_r,
    g_s, g_r, wr_s, wr_r,
):
    seq = lax.axis_index("seq")
    core = lax.axis_index("head")
    x = lax.rem(seq, NX)
    z = lax.div(seq, NX)

    def x_peer(d):
        return lax.rem(x + d, NX)

    def z_peer(d):
        return lax.rem(z + d, NZ)

    def at_x(d):
        return {"seq": z * NX + x_peer(d)}

    def at_z(d):
        return {"seq": z_peer(d) * NX + x}

    partner = {"head": 1 - core}

    barrier = pltpu.get_barrier_semaphore()
    for d in range(1, NX):
        pl.semaphore_signal(barrier, inc=1, device_id=at_x(d), device_id_type=MESH)
    for d in range(1, NZ):
        pl.semaphore_signal(barrier, inc=1, device_id=at_z(d), device_id_type=MESH)
    pl.semaphore_signal(barrier, inc=1, device_id=partner, device_id_type=MESH)

    dcopy = pltpu.make_async_copy(d_hbm, dec, lsem.at[0])
    dcopy.start()
    loads = []
    for n, src in enumerate((k_hbm, v_hbm, q_hbm)):
        for c in range(4):
            rows = pl.ds(c * TB, TB)
            loads.append(pltpu.make_async_copy(src.at[rows], raw.at[n, rows], lsem.at[1 + n]))
    for c in loads[:8]:
        c.start()
    gcopy = pltpu.make_async_copy(gate_hbm, gate, lsem.at[4])

    def arrived(ref, sem):
        pltpu.make_async_copy(ref, ref, sem).wait()

    def remote(src, dst, ss, rs, dev):
        return pltpu.make_async_remote_copy(
            src_ref=src, dst_ref=dst, send_sem=ss, recv_sem=rs, device_id=dev, device_id_type=MESH
        )

    own_cols = pl.ds(pl.multiple_of(core * COLS, COLS), COLS)
    other_cols = pl.ds(pl.multiple_of((1 - core) * COLS, COLS), COLS)
    w_local, w_far = [], []
    for h in range(HL):
        rows = pl.ds(h * DH, DH)
        w_local.append(
            pltpu.make_async_copy(
                w_hbm.at[rows, own_cols], wcat.at[pl.ds(h * 2 * DH, DH)], lsem.at[5]
            )
        )
        w_far.append(
            remote(
                w_hbm.at[rows, other_cols], wcat.at[pl.ds(h * 2 * DH + DH, DH)],
                wr_s.at[0], wr_r.at[h], partner,
            )
        )

    ri = lax.broadcasted_iota(jnp.int32, (256, 256), 0)
    ci = lax.broadcasted_iota(jnp.int32, (256, 256), 1)
    perm[...] = jnp.where(ci == HL * (ri % 64) + ri // 64, 1.0, 0.0).astype(BF)

    ui = lax.broadcasted_iota(jnp.int32, (128, 256), 0)
    uj = lax.broadcasted_iota(jnp.int32, (128, 256), 1)
    upper = jnp.where(ui <= uj, 1.0, 0.0).astype(F32)
    dcopy.wait()
    stacked = jnp.concatenate([dec[:, c * 128:(c + 1) * 128] for c in range(8)], axis=0)
    sums = jnp.dot(stacked, upper, precision=lax.Precision.HIGHEST, preferred_element_type=F32)
    off = jnp.zeros((HL, 128), F32)
    parts = []
    for c in range(8):
        parts.append(-(off + sums[c * HL:(c + 1) * HL, :128]))
        off = off + sums[c * HL:(c + 1) * HL, 128:]
    w4 = jnp.concatenate(parts, axis=1)
    tot = -off
    tot8 = jnp.concatenate([tot] * 8, axis=1)
    ek = jnp.exp(tot8 - w4)
    eq = jnp.exp(w4)
    rows16 = jnp.concatenate([w4, ek, eq, eq], axis=0)
    wrow[...] = rows16
    wcol[...] = rows16.T
    tt = jnp.concatenate([tot, tot], axis=1)
    tsend[...] = jnp.concatenate([tt, tt], axis=0)
    txr[x] = tsend[...]

    def permute(n, dst, scaled=None):
        arrived(raw.at[n], lsem.at[1 + n])
        for b in range(TOK // 64):
            p0 = b * 64
            r = jnp.dot(
                perm[...], raw[n, p0:p0 + 64].reshape(256, 256), preferred_element_type=F32
            )
            for h in range(HL):
                rh = r[h * 64:(h + 1) * 64]
                dst[h, p0:p0 + 64, :] = rh.astype(BF)
                if scaled is not None:
                    scaled[h, p0:p0 + 64, :] = (rh * wcol[p0:p0 + 64, HL + h:HL + h + 1]).astype(BF)

    with SC("permk"):
        permute(0, kp, ks)
    with SC("permv"):
        permute(1, vp)
    for c in loads[8:]:
        c.start()
    gcopy.start()

    def state(h):
        value = lax.dot_general(
            ks[h], vp[h], (((0,), (0,)), ((), ())), preferred_element_type=F32
        ).astype(BF)
        for r in range(NX):
            sb[h, r] = value[r * QR:(r + 1) * QR]
        xs[h, x] = sb[h, x]

    def send_state(h):
        for d in (1, 3, 2):
            remote(sb.at[h, x_peer(d)], xs.at[h, x], s1_s.at[0], s1_r.at[h], at_x(d)).start()

    with SC("state0"):
        state(0)
    with SC("barrier"):
        pl.semaphore_wait(barrier, NX - 1 + NZ - 1 + 1)
    for d in range(1, NX):
        remote(tsend, txr.at[x], tx_s.at[0], tx_r.at[0], at_x(d)).start()
    send_state(0)
    with SC("state123"):
        for h in range(1, HL):
            state(h)
            send_state(h)
    with SC("permq"):
        permute(2, qp)
    for h in range(HL):
        w_local[h].start()
    w_far[0].start()

    def row_totals():
        with SC("txwait"):
            arrived(txr.at[pl.ds(0, NX - 1)], tx_r.at[0])
        row_total = txr[0] + txr[1] + txr[2] + txr[3]
        tzsend[...] = row_total
        tzr[z] = row_total
        etx[...] = jnp.exp(txr[...])
        for d in range(1, NZ):
            remote(tzsend, tzr.at[z], tz_s.at[0], tz_r.at[0], at_z(d)).start()

    ti = lax.broadcasted_iota(jnp.int32, (TB, TB), 0)
    si = lax.broadcasted_iota(jnp.int32, (TB, TB), 1)

    def do_within(h):
        for tb in range(TOK // TB):
            t0 = tb * TB
            n = t0 + TB
            s = lax.dot_general(
                qp[h, t0:n, :], kp[h, :n, :], (((1,), (1,)), ((), ())), preferred_element_type=F32
            )
            wt = wcol[t0:n, h:h + 1]
            diag = jnp.where(ti >= si, wt - wrow[h:h + 1, t0:n], -jnp.inf)
            p = (s[:, t0:] * jnp.exp(diag)).astype(BF)
            if tb > 0:
                far = (s[:, :t0] * jnp.exp(wt - wrow[h:h + 1, :t0])).astype(BF)
                p = jnp.concatenate([far, p], axis=1)
            within[h, t0:n, :] = jnp.dot(p, vp[h, :n, :], preferred_element_type=F32)

    def stage_a(h):
        with SC(f"Await{h}"):
            arrived(xs.at[h, pl.ds(0, NX - 1)], s1_r.at[h])
        a = xs[h, 0].astype(F32)
        for i in range(1, NX):
            a = a * etx[i, h:h + 1, :] + xs[h, i].astype(F32)
        a = a.astype(BF)
        for r in range(4):
            for c in range(2):
                ab[h, r + 4 * c] = a[r * PR:(r + 1) * PR, c * PC:(c + 1) * PC]
        zr[h, z] = ab[h, z]
        for d in (4, 3, 5, 2, 6, 1, 7):
            remote(ab.at[h, z_peer(d)], zr.at[h, z], s2_s.at[0], s2_r.at[h], at_z(d)).start()

    def stage_z(h):
        with SC(f"Zwait{h}"):
            arrived(zr.at[h, pl.ds(0, NZ - 1)], s2_r.at[h])
        run = zr[h, 0].astype(F32)
        i0s[h, 0] = jnp.zeros((PR, PC), BF)
        i0s[h, 1] = run.astype(BF)
        for i in range(1, NZ - 1):
            run = run * etz[i, h:h + 1, :PC] + zr[h, i].astype(F32)
            i0s[h, i + 1] = run.astype(BF)
        i0r[h, z] = i0s[h, z]
        for d in (4, 3, 5, 2, 6, 1, 7):
            remote(i0s.at[h, z_peer(d)], i0r.at[h, z], s3_s.at[0], s3_r.at[h], at_z(d)).start()

    def stage_x(h):
        with SC(f"Xwait{h}"):
            arrived(i0r.at[h, pl.ds(0, NZ - 1)], s3_r.at[h])
        for r in range(4):
            for c in range(2):
                rows, cols = slice(r * PR, (r + 1) * PR), slice(c * PC, (c + 1) * PC)
                run = i0r[h, r + 4 * c].astype(F32)
                ins[h, 0, rows, cols] = run.astype(BF)
                for i in range(NX - 1):
                    run = run * etx[i, h:h + 1, cols] + xs[h, i, rows, cols].astype(F32)
                    ins[h, i + 1, rows, cols] = run.astype(BF)
        inr[h, x] = ins[h, x]
        for d in (2, 1, 3):
            remote(ins.at[h, x_peer(d)], inr.at[h, x], s4_s.at[0], s4_r.at[h], at_x(d)).start()

    for h in range(HL):
        with SC(f"within{h}"):
            do_within(h)
        if h == 0:
            row_totals()
        stage_a(h)
        if h == 0:
            w_far[1].start()

    with SC("tzwait"):
        arrived(tzr.at[pl.ds(0, NZ - 1)], tz_r.at[0])
    etz[...] = jnp.exp(tzr[...])

    gcopy.wait()

    def gate_factor(h):
        cols = slice(h * DH, (h + 1) * DH)
        gp = gate[:, cols].astype(F32)
        gfac[:, cols] = gain_ref[:, cols] * (gp / (1.0 + jnp.exp(-gp)))

    for h in range(HL):
        with SC(f"gate{h}"):
            gate_factor(h)
        stage_z(h)
        if h == 0:
            w_far[2].start()
    for h in range(HL):
        stage_x(h)
        if h == 0:
            w_far[3].start()

    def incoming_wait(h):
        with SC(f"Fwait{h}"):
            arrived(inr.at[h, pl.ds(0, NX - 1)], s4_r.at[h])

    def finalize(h, tb):
        rows = slice(tb * TB, (tb + 1) * TB)
        inc = inr[h].reshape(DH, DH)
        ret = jnp.dot(qp[h, rows, :], inc, preferred_element_type=F32)
        ret = ret * wcol[rows, 2 * HL + h:2 * HL + h + 1] + within[h, rows, :]
        center = jnp.mean(ret, axis=1, keepdims=True)
        shifted = ret - center
        variance = jnp.mean(shifted * shifted, axis=1, keepdims=True)
        normed = shifted * lax.rsqrt(variance + 1e-06)
        gcat[rows, h * 2 * DH:h * 2 * DH + DH] = (
            normed * gfac[rows, h * DH:(h + 1) * DH]
        ).astype(BF)

    def exchange(h):
        remote(
            gcat.at[:, pl.ds(h * 2 * DH, DH)], gcat.at[:, pl.ds(h * 2 * DH + DH, DH)],
            g_s.at[0], g_r.at[h], partner,
        ).start()

    def partner_wait(h):
        with SC(f"pwait{h}"):
            w_far[h].wait_recv()
            arrived(gcat.at[:, pl.ds(h * 2 * DH + DH, DH)], g_r.at[h])

    def project(n, j):
        depth = slice(max(2 * n - 1, 0) * DH, min(2 * n + 1, 2 * HL) * DH)
        cols = slice(j * 256, (j + 1) * 256)
        part = jnp.dot(gcat[:, depth], wcat[depth, cols], preferred_element_type=F32)
        if n == 0:
            acc[:, cols] = part
        elif n < HL:
            acc[:, cols] += part
        else:
            o_ref[:, cols] = (acc[:, cols] + part).astype(BF)

    blocks = TOK // TB
    incoming_wait(0)
    with SC("finalize0"):
        for tb in range(blocks):
            finalize(0, tb)
    exchange(0)
    arrived(wcat.at[pl.ds(0, HL * DH)], lsem.at[5])
    for n in range(HL + 1):
        if n > 0:
            partner_wait(n - 1)
        if n + 1 < HL:
            incoming_wait(n + 1)
        with SC(f"project{n}"):
            for j in range(COLS // 256):
                project(n, j)
                if n + 1 < HL and j % 2 == 1:
                    finalize(n + 1, j // 2)
        if n + 1 < HL:
            exchange(n + 1)

    with SC("sendwait"):
        arrived(sb.at[:, pl.ds(0, NX - 1)], s1_s.at[0])
        arrived(ab.at[:, pl.ds(0, NZ - 1)], s2_s.at[0])
        arrived(i0s.at[:, pl.ds(0, NZ - 1)], s3_s.at[0])
        arrived(ins.at[:, pl.ds(0, NX - 1)], s4_s.at[0])
        arrived(txr.at[pl.ds(0, NX - 1)], tx_s.at[0])
        arrived(tzr.at[pl.ds(0, NZ - 1)], tz_s.at[0])
        arrived(wcat.at[pl.ds(0, HL * DH)], wr_s.at[0])
        arrived(gcat.at[:, pl.ds(0, HL * DH)], g_s.at[0])


def on_device(queries, keys, content_vectors, decay_rate, gate_pre, norm_gain, out_weight):
    hbm = pl.BlockSpec(memory_space=pl.ANY)
    vmem = pl.BlockSpec(memory_space=pltpu.VMEM)
    dma = pltpu.SemaphoreType.DMA
    scratch = [
        pltpu.VMEM((3, TOK, HL, DH), BF),
        pltpu.VMEM((HL, TOK, DH), BF),
        pltpu.VMEM((HL, TOK, DH), BF),
        pltpu.VMEM((HL, TOK, DH), BF),
        pltpu.VMEM((HL, TOK, DH), BF),
        pltpu.VMEM((HL, TOK), F32),
        pltpu.VMEM((TOK, HL * DH), BF),
        pltpu.VMEM((TOK, HL * DH), F32),
        pltpu.VMEM((2 * HL * DH, COLS), BF),
        pltpu.VMEM((TOK, 2 * HL * DH), BF),
        pltpu.VMEM((TOK, COLS), F32),
        pltpu.VMEM((HL, TOK, DH), F32),
        pltpu.VMEM((256, 256), BF),
        pltpu.VMEM((4 * HL, TOK), F32),
        pltpu.VMEM((TOK, 4 * HL), F32),
        pltpu.VMEM((HL, NX, QR, DH), BF),
        pltpu.VMEM((HL, NX, QR, DH), BF),
        pltpu.VMEM((HL, NZ, PR, PC), BF),
        pltpu.VMEM((HL, NZ, PR, PC), BF),
        pltpu.VMEM((HL, NZ, PR, PC), BF),
        pltpu.VMEM((HL, NZ, PR, PC), BF),
        pltpu.VMEM((HL, NX, QR, DH), BF),
        pltpu.VMEM((HL, NX, QR, DH), BF),
        pltpu.VMEM((8, DH), F32),
        pltpu.VMEM((NX, 8, DH), F32),
        pltpu.VMEM((NX, 8, DH), F32),
        pltpu.VMEM((8, DH), F32),
        pltpu.VMEM((NZ, 8, DH), F32),
        pltpu.VMEM((NZ, 8, DH), F32),
        dma((6,)), dma((1,)), dma((1,)), dma((1,)), dma((1,)),
        dma((1,)), dma((HL,)), dma((1,)), dma((HL,)),
        dma((1,)), dma((HL,)), dma((1,)), dma((HL,)),
        dma((1,)), dma((HL,)), dma((1,)), dma((HL,)),
    ]
    return pl.pallas_call(
        kernel,
        out_shape=pltpu.VMEM((TOK, COLS), BF),
        in_specs=[hbm, hbm, hbm, hbm, hbm, vmem, hbm],
        out_specs=vmem,
        scratch_shapes=scratch,
        compiler_params=pltpu.CompilerParams(
            collective_id=0, has_side_effects=True, vmem_limit_bytes=VMEM_MIB * 1024 * 1024
        ),
        name="retention",
    )(queries, keys, content_vectors, decay_rate, gate_pre, norm_gain.reshape(1, -1), out_weight)


def solution(mesh):
    in_specs = (
        P(("batch", "seq"), "head", None),
        P(("batch", "seq"), "head", None),
        P(("batch", "seq"), "head", None),
        P("head", ("batch", "seq")),
        P(("batch", "seq"), "head"),
        P("head"),
        P("head", None),
    )
    out_specs = P(("batch", "seq"), "head")
    return jax.shard_map(
        on_device, mesh=mesh, in_specs=in_specs, out_specs=out_specs, check_vma=False
    )
```

time: 54 us -> 43.5 us (0.81)
  Pallas kernels: 49 us -> 41.3 us
  local copies, waits for them, and re-layouts: 4.79 us -> 2.02 us
    pallas_call x1, Pallas kernels: 49 us -> 41.3 us  [on_device(): pl.pallas_call(kernel, out_shape=pltpu.VMEM((TOK, COLS), BF), in_specs=[h...]
    unnamed x1, local copies, waits for them, and re-layouts: 4.79 us -> 2.02 us
where the time goes in v2:
time: 43.5 us; the launch traced here: 43.3 us
  Pallas kernels  41.3 us (95%)
  local copies, waits for them, and re-layouts  2.02 us (5%)
    pallas_call x1, Pallas kernels, on_device(): pl.pallas_call(kernel, out_shape=pltpu.VMEM((TOK, COLS), BF), in_specs=[h...  41.3 us
    unnamed x1, local copies, waits for them, and re-layouts  2.02 us

profile of v2, /device:TPU:1, one launch (start us, length us, event | category | flops | bytes accessed | tf_op | source)
XLA Modules:
  0.0 43.3 jit_solution(16336820643609594501)
XLA Ops:
  0.0 41.3 %retention.1 = bf16[1024,2048]{1,0:T(8,128)(2,1)S(1)} custom-call(bf16[1024,4,256]{2,1,0:T(4,128)(2,1)} %q_hbm.1, bf16[1024,4,256]{2,1,0:T(4,128)(2,1)} %k_hbm.1, bf16[1024,4,256]{2,1,0:T(4,128)(2,1)} %v_hbm.1, f32[4,1024]{1,0:T(4,128)} %d_hbm.1, bf16[1024,1024]{1,0:T(8,128)(2,1)} %gate_hbm.1, f32[1,1024]{1,0:T(1,128)} %bitcast.1, bf16[1024,4096]{1,0:T(8,128)(2,1)} %w_hbm.1), custom_call_target="tpu_custom_call" | custom-call | tf_op jit(solution)/shard_map/retention/pallas_call | solution.py:377
  41.3 2.0 %copy.9 = bf16[1024,2048]{1,0:T(8,128)(2,1)} copy(bf16[1024,2048]{1,0:T(8,128)(2,1)S(1)} %retention.1) | data formatting | bytes 8388608
